TPU v7x, 32 devices: a whole 2x2x4 slice. The times are simulated.
32 devices in a mesh: grp: 8 (over y, x, core), sp: 4 (over z).
Axes of the slice: x: 2, y: 2, z: 4, core: 2. Of those that a mesh axis runs over, the one named last changes fastest.
Arguments:
- latents: bfloat16 [8, 512, 3072], P('grp', 'sp'), may hold values from -6 to 6
- timestep: int32 [8], P('grp'), may hold values from 0 to 999
- w_mod: bfloat16 [256, 9216], replicated, may hold values from -0.375 to 0.375
- w_qkv: bfloat16 [4, 3072, 384], P('sp', 'grp'), may hold values from -2 to 2
- w_out: bfloat16 [4, 128, 3072], P('sp', 'grp'), may hold values from -0.5 to 0.5
Outputs:
- update: bfloat16 [8, 512, 3072], P('grp', 'sp')
All inputs are finite; a program needn't handle non-finite values.
Results may differ from a plain program's by a relative error of at most 0.012.
Values may be sent and summed in bfloat16 or wider, within the bound.
A program may use at most 128 MiB of HBM per device.

v0:
```python
import functools
import math

import jax
import jax.numpy as jnp
from jax import lax
from jax.experimental import pallas as pl
from jax.experimental.pallas import tpu as pltpu
from jax.sharding import PartitionSpec as P

MESH = pl.DeviceIdType.MESH
CHUNKS = 4


def embedding(timestep, freq):
    half_freq = freq // 2
    freqs = jnp.exp(-math.log(10000.0) * jnp.arange(half_freq, dtype=jnp.float32) / half_freq)
    angles = timestep.astype(jnp.float32)[:, None] * freqs[None, :]
    return jnp.cos(angles), jnp.sin(angles)


def kernel(
    n_grp,
    n_sp,
    lat_hbm,
    cos_ref,
    sin_ref,
    wmod_hbm,
    wqkv_hbm,
    wout_hbm,
    out_hbm,
    lat,
    wmod,
    mod,
    normed,
    wq,
    wo,
    q_buf,
    kv,
    att_mine,
    att_send,
    out_buf,
    loc_sem,
    wz_s,
    wz_r,
    wx_s,
    wx_r,
    wd_s,
    wd_r,
    oz_s,
    oz_r,
    ox_s,
    ox_r,
    od_s,
    od_r,
    lat_s,
    lat_r,
    kv_s,
    kv_r,
    at_s,
    at_r,
):
    g = lax.axis_index("grp")
    s = lax.axis_index("sp")
    core, chip = g % 2, g // 2
    chips = n_grp // 2
    pairs = n_sp // 2
    parity, pair = s % 2, s // 2
    tok, width = lat_hbm.shape[1], lat_hbm.shape[2]
    rows_q = wqkv_hbm.shape[1]
    rows_o = wout_hbm.shape[1]
    head = wqkv_hbm.shape[2] // 3
    sib = (chip * 2 + 1 - core, s)
    mate = (g, pair * 2 + 1 - parity)

    def at_chip(c):
        return ((chip + c) % chips * 2 + core, s)

    def at_pair(k, flip):
        return (g, (pair + k) % pairs * 2 + (parity + flip) % 2)

    def remote(src, dst, ssem, rsem, device):
        return pltpu.make_async_remote_copy(
            src_ref=src, dst_ref=dst, send_sem=ssem, recv_sem=rsem, device_id=device, device_id_type=MESH
        )

    def wq_rows(k, owner):
        return wq.at[k, pl.ds(pl.multiple_of(owner * rows_q, rows_q), rows_q), :]

    def wo_rows(par, k, owner):
        first = (par * pairs + k) * head + owner * rows_o
        return wo.at[pl.ds(pl.multiple_of(first, rows_o), rows_o), :]

    barrier = pltpu.get_barrier_semaphore()
    peers = [sib] + [at_chip(c) for c in range(1, chips)]
    peers += [at_pair(k, f) for k in range(pairs) for f in range(2) if (k, f) != (0, 0)]
    for peer in peers:
        pl.semaphore_signal(barrier, inc=1, device_id=peer, device_id_type=MESH)
    local = [
        pltpu.make_async_copy(wqkv_hbm.at[0], wq_rows(0, g), loc_sem.at[0]),
        pltpu.make_async_copy(wout_hbm.at[0], wo_rows(parity, 0, g), loc_sem.at[1]),
        pltpu.make_async_copy(lat_hbm.at[0], lat.at[0], loc_sem.at[2]),
        pltpu.make_async_copy(wmod_hbm, wmod, loc_sem.at[3]),
    ]
    for copy in local:
        copy.start()
    local[0].wait()
    local[1].wait()
    local[2].wait()
    pl.semaphore_wait(barrier, len(peers))

    sends = []

    def start(*args):
        copy = remote(*args)
        copy.start()
        sends.append(copy)

    def arrive(region, ssem, rsem):
        remote(region, region, ssem, rsem, sib).wait_recv()

    square = chips == 4
    near_x = chip // 2 * 2 + 1 - chip % 2
    near_y = (chip + 2) % 4
    corner = (near_x + 2) % 4
    to_x, to_y = (near_x * 2 + core, s), (near_y * 2 + core, s)
    others = [near_x, near_y, corner] if square else [(chip + chips - c) % chips for c in range(1, chips)]

    def q_part(k, owner, half):
        size = rows_q // 2
        return wq.at[k, pl.ds(pl.multiple_of(owner * rows_q + half * size, size), size), :]

    def o_part(par, k, owner, half):
        first = (par * pairs + k) * head + owner * rows_o
        size = width // 2
        return wo.at[pl.ds(pl.multiple_of(first, rows_o), rows_o), half * size : (half + 1) * size]

    class Spread:
        def __init__(self, i, whole, part, xs, xr, ds, dr):
            self.i, self.whole, self.part = i, whole, part
            self.xs, self.xr, self.ds, self.dr = xs, xr, ds, dr

        def cross(self, region, slot, device):
            start(region, region, self.xs.at[self.i, slot], self.xr.at[self.i, slot], device)

        def land(self, region, slot):
            arrive(region, self.xs.at[self.i, slot], self.xr.at[self.i, slot])

        def to_sib(self, region, slot):
            start(region, region, self.ds.at[self.i, slot], self.dr.at[self.i, slot], sib)

        def begin(self):
            mine = self.whole(g)
            if square:
                self.cross(mine, 0, to_x)
                self.cross(mine, 1, to_y)
            else:
                for c in range(1, chips):
                    self.cross(mine, c - 1, at_chip(c))
            self.to_sib(mine, 0)

        def relay(self):
            if square:
                for slot, device in ((0, to_y), (1, to_x)):
                    owner = others[slot] * 2 + core
                    self.land(self.whole(owner), slot)
                    self.cross(self.part(owner, slot), 2 + slot, device)
                    self.to_sib(self.whole(owner), 1 + slot)
            else:
                for slot in range(chips - 1):
                    region = self.whole(others[slot] * 2 + core)
                    self.land(region, slot)
                    self.to_sib(region, 1 + slot)

        def last(self):
            if square:
                owner = corner * 2 + core
                self.land(self.part(owner, 0), 2)
                self.land(self.part(owner, 1), 3)
                self.to_sib(self.whole(owner), 3)

        def finish(self):
            for slot, owner in enumerate([chip] + others):
                arrive(self.whole(owner * 2 + 1 - core), self.ds.at[self.i, slot], self.dr.at[self.i, slot])

    def spread_q(k):
        return Spread(k, functools.partial(wq_rows, k), functools.partial(q_part, k), wx_s, wx_r, wd_s, wd_r)

    def spread_o(k, flip):
        par = (parity + flip) % 2
        whole, part = functools.partial(wo_rows, par, k), functools.partial(o_part, par, k)
        return Spread(k * 2 + flip, whole, part, ox_s, ox_r, od_s, od_r)

    far = [(k, f) for k in range(pairs) for f in range(2) if (k, f) != (0, 0)]
    all_q = [spread_q(k) for k in range(pairs)]
    near_o, far_o = spread_o(0, 0), [spread_o(k, f) for k, f in far]

    def land_o(n):
        k, f = far[n]
        i = k * 2 + f
        arrive(wo_rows((parity + f) % 2, k, g), oz_s.at[i], oz_r.at[i])
        far_o[n].begin()

    all_q[0].begin()
    for k in range(1, pairs):
        start(wq_rows(0, g), wq_rows(k, g), wz_s.at[k], wz_r.at[k], at_pair(k, 0))

    def send_o(n):
        for k, f in far[n : n + 1]:
            i = k * 2 + f
            start(wo_rows(parity, 0, g), wo_rows(parity, k, g), oz_s.at[i], oz_r.at[i], at_pair(k, f))

    piece = tok // CHUNKS

    def send_chunk(c):
        rows = pl.ds(c * piece, piece)
        start(lat.at[0, rows, :], lat.at[1, rows, :], lat_s.at[c], lat_r.at[c], mate)

    send_chunk(0)

    local[3].wait()
    step = min(512, width)
    embed = jnp.concatenate([cos_ref[...], sin_ref[...]], axis=1).astype(jnp.bfloat16)
    embed = jnp.broadcast_to(embed, (16, embed.shape[1]))

    @pl.loop(0, 3 * width // step)
    def _(i):
        cols = pl.ds(pl.multiple_of(i * step, step), step)
        part = jnp.dot(embed, wmod[:, cols], preferred_element_type=jnp.float32)
        mod[:, cols] = part[:8]

    def normalize(which, first, count):
        block = 16

        @pl.loop(0, count // block)
        def _(i):
            rows = pl.ds(pl.multiple_of(first + i * block, block), block)
            values = lat[which, rows, :].astype(jnp.float32)
            center = jnp.mean(values, axis=-1, keepdims=True)
            values = values - center
            spread = jnp.mean(values * values, axis=-1, keepdims=True)
            scaled = values * lax.rsqrt(spread + 1e-06)
            shift = mod[0:1, 0:width]
            scale = mod[0:1, width : 2 * width]
            target = pl.ds(pl.multiple_of(which * tok + first + i * block, block), block)
            normed[target, :] = (scaled * (1.0 + scale) + shift).astype(jnp.bfloat16)

    def normalize_chunk(c):
        region = lat.at[1, pl.ds(c * piece, piece), :]
        arrive(region, lat_s.at[c], lat_r.at[c])
        normalize(1, c * piece, piece)

    spans = [(0, tok), (tok, tok - piece), (2 * tok - piece, piece)]

    def project(k, part):
        rows = pl.ds(*spans[part])
        result = jnp.dot(normed[rows, :], wq[k], preferred_element_type=jnp.float32).astype(jnp.bfloat16)
        q_buf[k, rows, :] = result[:, :head]
        kv[0, k, rows, :] = result[:, head:]

    def share_kv(k, part):
        rows = pl.ds(*spans[part])
        for d in range(1, pairs):
            there = (k + d) % pairs
            start(kv.at[0, k, rows, :], kv.at[d, there, rows, :], kv_s.at[d, k, part], kv_r.at[d, there, part], at_pair(d, 0))

    normalize(0, 0, tok)
    all_q[0].relay()
    near_o.begin()
    send_chunk(1)
    for k in range(1, pairs):
        arrive(wq_rows(k, g), wz_s.at[k], wz_r.at[k])
        all_q[k].begin()
    send_o(0)
    send_chunk(2)
    send_o(1)
    send_chunk(3)
    for n in range(2, len(far)):
        send_o(n)
    all_q[0].last()
    near_o.relay()
    all_q[0].finish()
    project(0, 0)
    share_kv(0, 0)
    near_o.last()
    for k in range(1, pairs):
        all_q[k].relay()
    normalize_chunk(0)
    for k in range(1, pairs):
        all_q[k].last()
        all_q[k].finish()
        project(k, 0)
        share_kv(k, 0)
    land_o(0)
    land_o(1)
    for c in range(1, CHUNKS - 1):
        normalize_chunk(c)
    for k in range(pairs):
        project(k, 1)
        share_kv(k, 1)
    normalize_chunk(CHUNKS - 1)
    for k in range(pairs):
        project(k, 2)
        share_kv(k, 2)
    far_o[0].relay()
    for n in range(2, len(far)):
        land_o(n)
    far_o[1].relay()
    far_o[0].last()

    def attend(k):
        for d in range(1, pairs):
            for part, span in enumerate(spans):
                arrive(kv.at[d, k, pl.ds(*span), :], kv_s.at[d, k, part], kv_r.at[d, k, part])
        total = pairs * 2 * tok
        keys = kv[:, k, :, :head].reshape(total, head)
        values = kv[:, k, :, head:].reshape(total, head)
        cols = pl.ds(pl.multiple_of((parity * pairs + k) * head, head), head)
        for which in (1, 0):
            query = q_buf[k, pl.ds(which * tok, tok), :]
            scores = lax.dot_general(query, keys, (((1,), (1,)), ((), ())), preferred_element_type=jnp.float32)
            scores = scores / math.sqrt(head)
            largest = jnp.max(scores, axis=1, keepdims=True)
            weights = jnp.exp(scores - largest)
            probs = (weights / jnp.sum(weights, axis=1, keepdims=True)).astype(jnp.bfloat16)
            result = jnp.dot(probs, values, preferred_element_type=jnp.float32).astype(jnp.bfloat16)
            if which == 1:
                att_send[k] = result
                start(att_send.at[k], att_mine.at[:, cols], at_s.at[k], at_r.at[k], mate)
            else:
                att_mine[:, cols] = result

    attend(0)
    for spread in far_o[2:]:
        spread.relay()
    far_o[1].last()
    for k in range(1, pairs):
        attend(k)
    for spread in far_o[2:]:
        spread.last()
    for spread in [near_o] + far_o:
        spread.finish()
    for k in range(pairs):
        cols = pl.ds(pl.multiple_of(((1 - parity) * pairs + k) * head, head), head)
        arrive(att_mine.at[:, cols], at_s.at[k], at_r.at[k])
    outs = []
    for i in range(width // step):
        cols = slice(i * step, (i + 1) * step)
        total = jnp.dot(att_mine[...], wo[:, cols], preferred_element_type=jnp.float32)
        gate = mod[0:1, 2 * width + i * step : 2 * width + (i + 1) * step]
        out_buf[:, cols] = (gate * total).astype(jnp.bfloat16)
        outs.append(pltpu.make_async_copy(out_buf.at[:, cols], out_hbm.at[0, :, cols], loc_sem.at[4 + i]))
        outs[i].start()
    for copy in outs:
        copy.wait()
    for copy in sends:
        copy.wait_send()


def on_device(n_grp, n_sp, latents, timestep, w_mod, w_qkv, w_out):
    _, tok, width = latents.shape
    freq = w_mod.shape[0]
    head = w_qkv.shape[2] // 3
    pairs, chips = n_sp // 2, n_grp // 2
    cos, sin = embedding(timestep, freq)
    dma = pltpu.SemaphoreType.DMA
    bf16 = jnp.bfloat16
    anywhere = pl.BlockSpec(memory_space=pl.ANY)
    vmem = pl.BlockSpec(memory_space=pltpu.VMEM)
    return pl.pallas_call(
        functools.partial(kernel, n_grp, n_sp),
        out_shape=jax.ShapeDtypeStruct(latents.shape, bf16),
        in_specs=[anywhere, vmem, vmem, anywhere, anywhere, anywhere],
        out_specs=anywhere,
        scratch_shapes=[
            pltpu.VMEM((2, tok, width), bf16),
            pltpu.VMEM(w_mod.shape, bf16),
            pltpu.VMEM((8, w_mod.shape[1]), jnp.float32),
            pltpu.VMEM((2 * tok, width), bf16),
            pltpu.VMEM((pairs, width, 3 * head), bf16),
            pltpu.VMEM((n_sp * head, width), bf16),
            pltpu.VMEM((pairs, 2 * tok, head), bf16),
            pltpu.VMEM((pairs, pairs, 2 * tok, 2 * head), bf16),
            pltpu.VMEM((tok, n_sp * head), bf16),
            pltpu.VMEM((pairs, tok, head), bf16),
            pltpu.VMEM((tok, width), bf16),
            dma((4 + width // min(512, width),)),
            dma((pairs,)),
            dma((pairs,)),
            dma((pairs, chips)),
            dma((pairs, chips)),
            dma((pairs, chips)),
            dma((pairs, chips)),
            dma((n_sp,)),
            dma((n_sp,)),
            dma((n_sp, chips)),
            dma((n_sp, chips)),
            dma((n_sp, chips)),
            dma((n_sp, chips)),
            dma((CHUNKS,)),
            dma((CHUNKS,)),
            dma((pairs, pairs, 3)),
            dma((pairs, pairs, 3)),
            dma((pairs,)),
            dma((pairs,)),
        ],
        compiler_params=pltpu.CompilerParams(
            collective_id=0, has_side_effects=True, vmem_limit_bytes=64000000
        ),
    )(latents, cos, sin, w_mod, w_qkv, w_out)


def solution(mesh):
    placed = (P("grp", "sp", None), P("grp"), P(), P("sp", "grp", None), P("sp", "grp", None))
    body = functools.partial(on_device, mesh.shape["grp"], mesh.shape["sp"])
    return jax.shard_map(
        body, mesh=mesh, in_specs=placed, out_specs=P("grp", "sp", None), check_vma=False
    )
```

profile of v0, /device:TPU:0, one launch (start us, length us, event | category | flops | bytes accessed | tf_op | source)
XLA Modules:
  0.0 57.2 jit_solution(4594385823026354209)
XLA Ops:
  0.7 0.6 %fusion = (f32[1,128]{1,0:T(1,128)}, f32[1,128]{1,0:T(1,128)}) fusion(f32[]{:T(128)} %bitcast), kind=kLoop, calls=%fused_computation.1 | loop fusion | flops 256 | bytes 1028 | tf_op jit(solution)/shard_map/sin | solution.py:19
  1.3 53.9 %shard_map.55 = bf16[1,128,3072]{2,1,0:T(8,128)(2,1)} custom-call(bf16[1,128,3072]{2,1,0:T(8,128)(2,1)} %lat_hbm.1, f32[1,128]{1,0:T(1,128)} %get-tuple-element.6.cos_ref, f32[1,128]{1,0:T(1,128)} %get-tuple-element.5.sin_ref, bf16[256,9216]{1,0:T(8,128)(2,1)} %wmod_hbm.1, bf16[1,384,384]{2,1,0:T(8,128)(2,1)} %wqkv_hbm.1, bf16[1,16,3072]{2,1,0:T(8,128)(2,1)} %wout_hbm.1), custom_call_target="tpu_custom_call" | custom-call | tf_op jit(solution)/shard_map/pallas_call | solution.py:370
  55.2 2.1 %copy.8 = bf16[1,128,3072]{2,1,0:T(8,128)(2,1)} copy(bf16[1,128,3072]{2,1,0:T(8,128)(2,1)} %shard_map.55) | data formatting | bytes 1572864
where the time goes:
time: 58.2 us; the launch traced here: 57.2 us
  Pallas kernels  53.9 us (93%)
  local copies, waits for them, and re-layouts  2.06 us (4%)
  between operations  0.66 us (1%)
  other arithmetic  0.6 us (1%)
    pallas_call x1, Pallas kernels, on_device(): pl.pallas_call(functools.partial(kernel, n_grp, n_sp), out_shape=jax.Shap...  53.9 us
    unnamed x1, local copies, waits for them, and re-layouts  2.06 us

commit v1 on v0

v1 whole, which is shorter than its diff:
```python
import functools
import math

import jax
import jax.numpy as jnp
from jax import lax
from jax.experimental import pallas as pl
from jax.experimental.pallas import tpu as pltpu
from jax.sharding import PartitionSpec as P

MESH = pl.DeviceIdType.MESH
CHUNKS = 4
LIMIT = 40 * 2**20


def embedding(timestep, freq):
    half_freq = freq // 2
    steps = lax.broadcasted_iota(jnp.int32, (8, half_freq), 1).astype(jnp.float32)
    angles = timestep.astype(jnp.float32) * jnp.exp(-math.log(10000.0) * steps / half_freq)
    return jnp.concatenate([jnp.cos(angles), jnp.sin(angles)], axis=1).astype(jnp.bfloat16)


def kernel(
    n_grp,
    n_sp,
    step_now,
    lat_hbm,
    wmod_hbm,
    wqkv_hbm,
    wout_hbm,
    att_mine,
    wo,
    mod,
    lat,
    wmod,
    normed,
    wq,
    q_buf,
    kv,
    att_send,
    loc_sem,
    q_s,
    o_s,
    lat_s,
    kv_s,
    at_s,
    wz_r,
    wx_r,
    wd_r,
    oz_r,
    ox_r,
    od_r,
    lat_r,
    kv_r,
    at_r,
):
    g = lax.axis_index("grp")
    s = lax.axis_index("sp")
    core, chip = g % 2, g // 2
    chips = n_grp // 2
    pairs = n_sp // 2
    parity, pair = s % 2, s // 2
    tok, width = lat_hbm.shape[1], lat_hbm.shape[2]
    rows_q = wqkv_hbm.shape[1]
    rows_o = wout_hbm.shape[1]
    head = wqkv_hbm.shape[2] // 3
    sib = (chip * 2 + 1 - core, s)
    mate = (g, pair * 2 + 1 - parity)

    def at_chip(c):
        return ((chip + c) % chips * 2 + core, s)

    def at_pair(k, flip):
        return (g, (pair + k) % pairs * 2 + (parity + flip) % 2)

    def remote(src, dst, ssem, rsem, device):
        return pltpu.make_async_remote_copy(
            src_ref=src, dst_ref=dst, send_sem=ssem, recv_sem=rsem, device_id=device, device_id_type=MESH
        )

    def wq_rows(k, owner):
        return wq.at[pl.ds(pl.multiple_of(k * width + owner * rows_q, rows_q), rows_q), :]

    def wo_rows(par, k, owner):
        first = (par * pairs + k) * head + owner * rows_o
        return wo.at[pl.ds(pl.multiple_of(first, rows_o), rows_o), :]

    barrier = pltpu.get_barrier_semaphore()
    peers = [sib] + [at_chip(c) for c in range(1, chips)]
    peers += [at_pair(k, f) for k in range(pairs) for f in range(2) if (k, f) != (0, 0)]
    for peer in peers:
        pl.semaphore_signal(barrier, inc=1, device_id=peer, device_id_type=MESH)
    local = [
        pltpu.make_async_copy(wqkv_hbm.at[0], wq_rows(0, g), loc_sem.at[0]),
        pltpu.make_async_copy(wout_hbm.at[0], wo_rows(parity, 0, g), loc_sem.at[1]),
        pltpu.make_async_copy(lat_hbm.at[0], lat.at[0], loc_sem.at[2]),
        pltpu.make_async_copy(wmod_hbm, wmod, loc_sem.at[3]),
    ]
    for copy in local:
        copy.start()
    local[0].wait()
    local[1].wait()
    local[2].wait()
    pl.semaphore_wait(barrier, len(peers))

    sent = {"q": 0, "o": 0}

    def start(src, dst, ssem, rsem, device, kind=None):
        remote(src, dst, ssem, rsem, device).start()
        if kind is not None:
            sent[kind] += math.prod(src.shape)

    def arrive(region, ssem, rsem):
        remote(region, region, ssem, rsem, sib).wait_recv()

    square = chips == 4
    near_x = chip // 2 * 2 + 1 - chip % 2
    near_y = (chip + 2) % 4
    corner = (near_x + 2) % 4
    to_x, to_y = (near_x * 2 + core, s), (near_y * 2 + core, s)
    others = [near_x, near_y, corner] if square else [(chip + chips - c) % chips for c in range(1, chips)]

    def q_part(k, owner, half):
        size = rows_q // 2
        return wq.at[pl.ds(pl.multiple_of(k * width + owner * rows_q + half * size, size), size), :]

    def o_part(par, k, owner, half):
        first = (par * pairs + k) * head + owner * rows_o
        size = width // 2
        return wo.at[pl.ds(pl.multiple_of(first, rows_o), rows_o), half * size : (half + 1) * size]

    class Spread:
        def __init__(self, kind, i, whole, part, ssem, xr, dr):
            self.kind, self.i, self.whole, self.part = kind, i, whole, part
            self.ssem, self.xr, self.dr = ssem, xr, dr

        def cross(self, region, slot, device):
            start(region, region, self.ssem, self.xr.at[self.i, slot], device, self.kind)

        def land(self, region, slot):
            arrive(region, self.ssem, self.xr.at[self.i, slot])

        def to_sib(self, region):
            start(region, region, self.ssem, self.dr, sib, self.kind)

        def begin(self):
            mine = self.whole(g)
            if square:
                self.cross(mine, 0, to_x)
                self.cross(mine, 1, to_y)
            else:
                for c in range(1, chips):
                    self.cross(mine, c - 1, at_chip(c))
            self.to_sib(mine)

        def relay(self):
            if square:
                for slot, device in ((0, to_y), (1, to_x)):
                    owner = others[slot] * 2 + core
                    self.land(self.whole(owner), slot)
                    self.cross(self.part(owner, slot), 2 + slot, device)
                    self.to_sib(self.whole(owner))
            else:
                for slot in range(chips - 1):
                    region = self.whole(others[slot] * 2 + core)
                    self.land(region, slot)
                    self.to_sib(region)

        def last(self):
            if square:
                owner = corner * 2 + core
                self.land(self.part(owner, 0), 2)
                self.land(self.part(owner, 1), 3)
                self.to_sib(self.whole(owner))

    def spread_q(k):
        whole, part = functools.partial(wq_rows, k), functools.partial(q_part, k)
        return Spread("q", k, whole, part, q_s, wx_r, wd_r.at[k])

    def finish_q(k):
        arrive(wq.at[k * width : k * width + width // 2, :], q_s, wd_r.at[k])

    def spread_o(k, flip):
        par = (parity + flip) % 2
        whole, part = functools.partial(wo_rows, par, k), functools.partial(o_part, par, k)
        return Spread("o", k * 2 + flip, whole, part, o_s, ox_r, od_r)

    far = [(k, f) for k in range(pairs) for f in range(2) if (k, f) != (0, 0)]
    all_q = [spread_q(k) for k in range(pairs)]
    near_o, far_o = spread_o(0, 0), [spread_o(k, f) for k, f in far]

    def land_o(n):
        k, f = far[n]
        i = k * 2 + f
        arrive(wo_rows((parity + f) % 2, k, g), o_s, oz_r.at[i])
        far_o[n].begin()

    all_q[0].begin()
    for k in range(1, pairs):
        start(wq_rows(0, g), wq_rows(k, g), q_s, wz_r.at[k], at_pair(k, 0), "q")

    def send_o(n):
        for k, f in far[n : n + 1]:
            i = k * 2 + f
            start(wo_rows(parity, 0, g), wo_rows(parity, k, g), o_s, oz_r.at[i], at_pair(k, f), "o")

    piece = tok // CHUNKS

    def send_chunk(c):
        rows = pl.ds(c * piece, piece)
        start(lat.at[0, rows, :], lat.at[1, rows, :], lat_s, lat_r.at[c], mate)

    send_chunk(0)

    embed = embedding(step_now[0], wmod.shape[0])
    embed = jnp.concatenate([embed, embed], axis=0)
    local[3].wait()
    step = min(512, width)

    @pl.loop(0, 3 * width // step)
    def _(i):
        cols = pl.ds(pl.multiple_of(i * step, step), step)
        part = jnp.dot(embed, wmod[:, cols], preferred_element_type=jnp.float32)
        mod[:, cols] = part[:8]

    def normalize(which, first, count):
        block = 16

        @pl.loop(0, count // block)
        def _(i):
            rows = pl.ds(pl.multiple_of(first + i * block, block), block)
            values = lat[which, rows, :].astype(jnp.float32)
            center = jnp.mean(values, axis=-1, keepdims=True)
            values = values - center
            spread = jnp.mean(values * values, axis=-1, keepdims=True)
            scaled = values * lax.rsqrt(spread + 1e-06)
            shift = mod[0:1, 0:width]
            scale = mod[0:1, width : 2 * width]
            target = pl.ds(pl.multiple_of(which * tok + first + i * block, block), block)
            normed[target, :] = (scaled * (1.0 + scale) + shift).astype(jnp.bfloat16)

    def normalize_chunk(c):
        region = lat.at[1, pl.ds(c * piece, piece), :]
        arrive(region, lat_s, lat_r.at[c])
        normalize(1, c * piece, piece)

    spans = [(0, tok), (tok, tok - piece), (2 * tok - piece, piece)]

    def project(k, part):
        rows = pl.ds(*spans[part])
        result = jnp.dot(normed[rows, :], wq[k * width : (k + 1) * width, :], preferred_element_type=jnp.float32).astype(jnp.bfloat16)
        q_buf[k, rows, :] = result[:, :head]
        kv[0, k, rows, :] = result[:, head:]

    def share_kv(k, part):
        rows = pl.ds(*spans[part])
        for d in range(1, pairs):
            there = (k + d) % pairs
            start(kv.at[0, k, rows, :], kv.at[d, there, rows, :], kv_s, kv_r.at[d - 1, there], at_pair(d, 0))

    normalize(0, 0, tok)
    all_q[0].relay()
    near_o.begin()
    send_chunk(1)
    for k in range(1, pairs):
        arrive(wq_rows(k, g), q_s, wz_r.at[k])
        all_q[k].begin()
    send_o(0)
    send_chunk(2)
    send_o(1)
    send_chunk(3)
    for n in range(2, len(far)):
        send_o(n)
    all_q[0].last()
    near_o.relay()
    finish_q(0)
    project(0, 0)
    share_kv(0, 0)
    near_o.last()
    for k in range(1, pairs):
        all_q[k].relay()
    normalize_chunk(0)
    for k in range(1, pairs):
        all_q[k].last()
        finish_q(k)
        project(k, 0)
        share_kv(k, 0)
    land_o(0)
    land_o(1)
    for c in range(1, CHUNKS - 1):
        normalize_chunk(c)
    for k in range(pairs):
        project(k, 1)
        share_kv(k, 1)
    normalize_chunk(CHUNKS - 1)
    for k in range(pairs):
        project(k, 2)
        share_kv(k, 2)
    far_o[0].relay()
    for n in range(2, len(far)):
        land_o(n)
    far_o[1].relay()
    far_o[0].last()

    def attend(k):
        for d in range(1, pairs):
            arrive(kv.at[d, k], kv_s, kv_r.at[d - 1, k])
        total = pairs * 2 * tok
        keys = kv[:, k, :, :head].reshape(total, head)
        values = kv[:, k, :, head:].reshape(total, head)
        cols = pl.ds(pl.multiple_of((parity * pairs + k) * head, head), head)
        for which in (1, 0):
            query = q_buf[k, pl.ds(which * tok, tok), :]
            scores = lax.dot_general(query, keys, (((1,), (1,)), ((), ())), preferred_element_type=jnp.float32)
            scores = scores / math.sqrt(head)
            largest = jnp.max(scores, axis=1, keepdims=True)
            weights = jnp.exp(scores - largest)
            probs = (weights / jnp.sum(weights, axis=1, keepdims=True)).astype(jnp.bfloat16)
            result = jnp.dot(probs, values, preferred_element_type=jnp.float32).astype(jnp.bfloat16)
            if which == 1:
                att_send[k] = result
                start(att_send.at[k], att_mine.at[:, cols], at_s, at_r, mate)
            else:
                att_mine[:, cols] = result

    attend(0)
    for spread in far_o[2:]:
        spread.relay()
    far_o[1].last()
    for k in range(1, pairs):
        attend(k)
    for spread in far_o[2:]:
        spread.last()
    arrive(wo.at[0 : n_sp * head // 2, :], o_s, od_r)
    arrive(att_send, at_s, at_r)

    def drain(region, ssem):
        remote(region, region, ssem, at_r, sib).wait_send()

    drain(wq.at[0 : sent["q"] // wq.shape[1], :], q_s)
    drain(wo.at[0 : sent["o"] // width, :], o_s)
    drain(lat.at[0], lat_s)
    for d in range(1, pairs):
        drain(kv.at[0], kv_s)
    drain(att_send, at_s)


def project_out(att, wo, mod, out_hbm, out_buf, sems):
    width = wo.shape[1]
    step = width // sems.shape[0]
    outs = []
    for i in range(sems.shape[0]):
        cols = slice(i * step, (i + 1) * step)
        total = jnp.dot(att[...], wo[:, cols], preferred_element_type=jnp.float32)
        gate = mod[0:1, 2 * width + i * step : 2 * width + (i + 1) * step]
        out_buf[:, cols] = (gate * total).astype(jnp.bfloat16)
        outs.append(pltpu.make_async_copy(out_buf.at[:, cols], out_hbm.at[0, :, cols], sems.at[i]))
        outs[i].start()
    for copy in outs:
        copy.wait()


def on_device(n_grp, n_sp, latents, timestep, w_mod, w_qkv, w_out):
    _, tok, width = latents.shape
    head = w_qkv.shape[2] // 3
    pairs, chips = n_sp // 2, n_grp // 2
    dma = pltpu.SemaphoreType.DMA
    bf16 = jnp.bfloat16
    anywhere = pl.BlockSpec(memory_space=pl.ANY)
    vmem = pl.BlockSpec(memory_space=pltpu.VMEM)
    args = [pltpu.with_memory_space_constraint(a, pltpu.HBM) for a in (latents, w_mod, w_qkv, w_out)]
    att, wo, mod = pl.pallas_call(
        functools.partial(kernel, n_grp, n_sp),
        out_shape=[
            pltpu.VMEM((tok, n_sp * head), bf16),
            pltpu.VMEM((n_sp * head, width), bf16),
            pltpu.VMEM((8, w_mod.shape[1]), jnp.float32),
        ],
        in_specs=[pl.BlockSpec(memory_space=pltpu.SMEM)] + [anywhere] * 4,
        out_specs=[vmem] * 3,
        scratch_shapes=[
            pltpu.VMEM((2, tok, width), bf16),
            pltpu.VMEM(w_mod.shape, bf16),
            pltpu.VMEM((2 * tok, width), bf16),
            pltpu.VMEM((pairs * width, 3 * head), bf16),
            pltpu.VMEM((pairs, 2 * tok, head), bf16),
            pltpu.VMEM((pairs, pairs, 2 * tok, 2 * head), bf16),
            pltpu.VMEM((pairs, tok, head), bf16),
            dma((4,)),
            dma,
            dma,
            dma,
            dma,
            dma,
            dma((pairs,)),
            dma((pairs, max(chips - 1, 4))),
            dma((pairs,)),
            dma((n_sp,)),
            dma((n_sp, max(chips - 1, 4))),
            dma,
            dma((CHUNKS,)),
            dma((max(pairs - 1, 1), pairs)),
            dma,
        ],
        compiler_params=pltpu.CompilerParams(collective_id=0, has_side_effects=True, vmem_limit_bytes=LIMIT),
    )(timestep, *args)
    return pl.pallas_call(
        project_out,
        out_shape=jax.ShapeDtypeStruct(latents.shape, bf16),
        in_specs=[vmem] * 3,
        out_specs=anywhere,
        scratch_shapes=[pltpu.VMEM((tok, width), bf16), dma((max(width // 512, 1),))],
        compiler_params=pltpu.CompilerParams(vmem_limit_bytes=8 * 2**20),
    )(att, wo, mod)


def solution(mesh):
    placed = (P("grp", "sp", None), P("grp"), P(), P("sp", "grp", None), P("sp", "grp", None))
    body = functools.partial(on_device, mesh.shape["grp"], mesh.shape["sp"])
    return jax.shard_map(
        body, mesh=mesh, in_specs=placed, out_specs=P("grp", "sp", None), check_vma=False
    )
```

time: 58.2 us -> 54.2 us (0.931); the launches traced: 57.2 us -> 54 us
  local copies, waits for them, and re-layouts: 2.06 us -> 0 us
  other arithmetic: 0.6 us -> 0 us
    unnamed x1 -> x0, local copies, waits for them, and re-layouts: 2.06 us -> none
    sin x1 -> x0, other arithmetic: 0.6 us -> none  [embedding(): return (jnp.cos(angles), jnp.sin(angles))]
    pallas_call x1 -> x2, Pallas kernels: 53.9 us -> 53.4 us  [the longest x1 52.1 us: on_device(): pl.pallas_call(functools.partial(kernel, n_grp, n_sp), out_shape=[pltpu.V...]
where the time goes in v1:
time: 54.2 us; the launch traced here: 54 us
  Pallas kernels  53.4 us (99%)
  between operations  0.66 us (1%)
    pallas_call x1, Pallas kernels, on_device(): pl.pallas_call(functools.partial(kernel, n_grp, n_sp), out_shape=[pltpu.V...  52.1 us
    pallas_call x1, Pallas kernels, on_device(): pl.pallas_call(project_out, out_shape=jax.ShapeDtypeStruct(latents.shape,...  1.3 us

profile of v1, /device:TPU:0, one launch (start us, length us, event | category | flops | bytes accessed | tf_op | source)
XLA Modules:
  0.0 54.0 jit_solution(4148126113921514727)
XLA Ops:
  0.7 52.1 %shard_map.55 = (bf16[128,512]{1,0:T(8,128)(2,1)S(1)}, bf16[512,3072]{1,0:T(8,128)(2,1)S(1)}, f32[8,9216]{1,0:T(8,128)S(1)}) custom-call(s32[1]{0:T(128)S(6)} %copy.6.step_now, bf16[1,128,3072]{2,1,0:T(8,128)(2,1)} %lat_hbm.1, bf16[256,9216]{1,0:T(8,128)(2,1)} %wmod_hbm.1, bf16[1,384,384]{2,1,0:T(8,128)(2,1)} %wqkv_hbm.1, bf16[1,16,3072]{2,1,0:T(8,128)(2,1)} %wout_hbm.1), custom_call_target="tpu_custom_call" | custom-call | tf_op jit(solution)/shard_map/pallas_call | solution.py:372
  52.7 1.3 %shard_map.56 = bf16[1,128,3072]{2,1,0:T(8,128)(2,1)} custom-call(bf16[128,512]{1,0:T(8,128)(2,1)S(1)} %get-tuple-element.8.att, bf16[512,3072]{1,0:T(8,128)(2,1)S(1)} %get-tuple-element.9.wo, f32[8,9216]{1,0:T(8,128)S(1)} %get-tuple-element.10.mod), custom_call_target="tpu_custom_call" | custom-call | tf_op jit(solution)/shard_map/pallas_call | solution.py:407

commit v2 on v1

v2 whole, which is shorter than its diff:
```python
import functools
import math

import jax
import jax.numpy as jnp
from jax import lax
from jax.experimental import pallas as pl
from jax.experimental.pallas import tpu as pltpu
from jax.sharding import PartitionSpec as P

MESH = pl.DeviceIdType.MESH
CHUNKS = 4
LIMIT = 40 * 2**20


def embedding(timestep, freq):
    half_freq = freq // 2
    steps = lax.broadcasted_iota(jnp.int32, (8, half_freq), 1).astype(jnp.float32)
    angles = timestep.astype(jnp.float32) * jnp.exp(-math.log(10000.0) * steps / half_freq)
    return jnp.concatenate([jnp.cos(angles), jnp.sin(angles)], axis=1).astype(jnp.bfloat16)


def kernel(
    n_grp,
    n_sp,
    step_now,
    lat_hbm,
    wmod_hbm,
    wqkv_hbm,
    wout_hbm,
    att_mine,
    wo,
    mod,
    lat,
    wmod,
    normed,
    wq,
    q_buf,
    kv,
    att_send,
    att_far,
    loc_sem,
    q_s,
    o_s,
    lat_s,
    kv_s,
    at_s,
    wz_r,
    wx_r,
    wd_r,
    oz_r,
    ox_r,
    od_r,
    lat_r,
    kv_r,
    at_r,
    x_r,
):
    g = lax.axis_index("grp")
    s = lax.axis_index("sp")
    core, chip = g % 2, g // 2
    chips = n_grp // 2
    pairs = n_sp // 2
    parity, pair = s % 2, s // 2
    tok, width = lat_hbm.shape[1], lat_hbm.shape[2]
    rows_q = wqkv_hbm.shape[1]
    rows_o = wout_hbm.shape[1]
    head = wqkv_hbm.shape[2] // 3
    sib = (chip * 2 + 1 - core, s)
    mate = (g, pair * 2 + 1 - parity)
    line = n_sp == 4
    inner = (parity + pair) % 2
    piece = tok // CHUNKS
    part_rows = tok - piece

    def at_chip(c):
        return ((chip + c) % chips * 2 + core, s)

    def at_pair(k, flip):
        return (g, (pair + k) % pairs * 2 + (parity + flip) % 2)

    def when_inner(body):
        pl.when(inner == 1)(body)

    def when_outer(body):
        pl.when(inner == 0)(body)

    def remote(src, dst, ssem, rsem, device):
        return pltpu.make_async_remote_copy(
            src_ref=src, dst_ref=dst, send_sem=ssem, recv_sem=rsem, device_id=device, device_id_type=MESH
        )

    def wq_rows(k, owner):
        return wq.at[pl.ds(pl.multiple_of(k * width + owner * rows_q, rows_q), rows_q), :]

    def wo_rows(par, k, owner):
        first = (par * pairs + k) * head + owner * rows_o
        return wo.at[pl.ds(pl.multiple_of(first, rows_o), rows_o), :]

    barrier = pltpu.get_barrier_semaphore()
    peers = [sib] + [at_chip(c) for c in range(1, chips)]
    peers += [at_pair(k, f) for k in range(pairs) for f in range(2) if (k, f) != (0, 0)]
    for peer in peers:
        pl.semaphore_signal(barrier, inc=1, device_id=peer, device_id_type=MESH)
    local = [
        pltpu.make_async_copy(wqkv_hbm.at[0], wq_rows(0, g), loc_sem.at[0]),
        pltpu.make_async_copy(wout_hbm.at[0], wo_rows(parity, 0, g), loc_sem.at[1]),
        pltpu.make_async_copy(lat_hbm.at[0], lat.at[0:tok, :], loc_sem.at[2]),
        pltpu.make_async_copy(wmod_hbm, wmod, loc_sem.at[3]),
    ]
    for copy in local:
        copy.start()
    local[0].wait()
    local[1].wait()
    local[2].wait()
    pl.semaphore_wait(barrier, len(peers))

    def start(src, dst, ssem, rsem, device):
        remote(src, dst, ssem, rsem, device).start()

    def arrive(region, ssem, rsem):
        remote(region, region, ssem, rsem, sib).wait_recv()

    square = chips == 4
    near_x = chip // 2 * 2 + 1 - chip % 2
    near_y = (chip + 2) % 4
    corner = (near_x + 2) % 4
    to_x, to_y = (near_x * 2 + core, s), (near_y * 2 + core, s)
    others = [near_x, near_y, corner] if square else [(chip + chips - c) % chips for c in range(1, chips)]

    def q_part(k, owner, half):
        size = rows_q // 2
        return wq.at[pl.ds(pl.multiple_of(k * width + owner * rows_q + half * size, size), size), :]

    def o_part(par, k, owner, half):
        first = (par * pairs + k) * head + owner * rows_o
        size = width // 2
        return wo.at[pl.ds(pl.multiple_of(first, rows_o), rows_o), half * size : (half + 1) * size]

    class Spread:
        def __init__(self, i, whole, part, ssem, xr, dr):
            self.i, self.whole, self.part = i, whole, part
            self.ssem, self.xr, self.dr = ssem, xr, dr

        def cross(self, region, slot, device):
            start(region, region, self.ssem, self.xr.at[self.i, slot], device)

        def land(self, region, slot):
            arrive(region, self.ssem, self.xr.at[self.i, slot])

        def to_sib(self, region):
            start(region, region, self.ssem, self.dr, sib)

        def begin(self):
            mine = self.whole(g)
            if square:
                self.cross(mine, 0, to_x)
                self.cross(mine, 1, to_y)
            else:
                for c in range(1, chips):
                    self.cross(mine, c - 1, at_chip(c))
            self.to_sib(mine)

        def relay(self):
            if square:
                for slot, device in ((0, to_y), (1, to_x)):
                    owner = others[slot] * 2 + core
                    self.land(self.whole(owner), slot)
                    self.cross(self.part(owner, slot), 2 + slot, device)
                    self.to_sib(self.whole(owner))
            else:
                for slot in range(chips - 1):
                    region = self.whole(others[slot] * 2 + core)
                    self.land(region, slot)
                    self.to_sib(region)

        def last(self):
            if square:
                owner = corner * 2 + core
                self.land(self.part(owner, 0), 2)
                self.land(self.part(owner, 1), 3)
                self.to_sib(self.whole(owner))

    def spread_q(k):
        whole, part = functools.partial(wq_rows, k), functools.partial(q_part, k)
        return Spread(k, whole, part, q_s, wx_r, wd_r.at[k])

    def finish_q(k):
        arrive(wq.at[k * width : k * width + width // 2, :], q_s, wd_r.at[k])

    def spread_o(k, flip):
        par = (parity + flip) % 2
        whole, part = functools.partial(wo_rows, par, k), functools.partial(o_part, par, k)
        return Spread(k * 2 + flip, whole, part, o_s, ox_r, od_r)

    far = [(k, f) for k in range(pairs) for f in range(2) if (k, f) != (0, 0)]
    all_q = [spread_q(k) for k in range(pairs)]
    near_o = spread_o(0, 0)

    def send_q():
        for k in range(1, pairs):
            start(wq_rows(0, g), wq_rows(k, g), q_s, wz_r.at[k], at_pair(k, 0))

    def pass_o(par, k_here, k_there, flip_there, device):
        start(wo_rows(par, k_here, g), wo_rows(par, k_there, g), o_s, oz_r.at[k_there * 2 + flip_there], device)

    def land_o(k, flip):
        arrive(wo_rows((parity + flip) % 2, k, g), o_s, oz_r.at[k * 2 + flip])

    def send_chunk(c):
        rows = c * piece
        start(lat.at[pl.ds(rows, piece), :], lat.at[pl.ds(tok + rows, piece), :], lat_s, lat_r.at[c], mate)

    def send_inner():
        start(lat.at[pl.ds(part_rows, piece), :], lat.at[pl.ds(2 * tok, piece), :], lat_s, x_r.at[0], at_pair(1, 1))

    step = min(512, width)

    def modulate():
        embed = embedding(step_now[0], wmod.shape[0])
        embed = jnp.concatenate([embed, embed], axis=0)
        local[3].wait()

        @pl.loop(0, 3 * width // step)
        def _(i):
            cols = pl.ds(pl.multiple_of(i * step, step), step)
            part = jnp.dot(embed, wmod[:, cols], preferred_element_type=jnp.float32)
            mod[:, cols] = part[:8]

    def normalize(first, count):
        block = 16

        @pl.loop(0, count // block)
        def _(i):
            rows = pl.ds(pl.multiple_of(first + i * block, block), block)
            values = lat[rows, :].astype(jnp.float32)
            center = jnp.mean(values, axis=-1, keepdims=True)
            values = values - center
            spread = jnp.mean(values * values, axis=-1, keepdims=True)
            scaled = values * lax.rsqrt(spread + 1e-06)
            shift = mod[0:1, 0:width]
            scale = mod[0:1, width : 2 * width]
            normed[rows, :] = (scaled * (1.0 + scale) + shift).astype(jnp.bfloat16)

    def land_chunk(c):
        arrive(lat.at[pl.ds(tok + c * piece, piece), :], lat_s, lat_r.at[c])

    def normalize_chunk(c):
        land_chunk(c)
        normalize(tok + c * piece, piece)

    def project(k, first, count):
        rows = pl.ds(first, count)
        weights = wq[k * width : (k + 1) * width, :]
        result = jnp.dot(normed[rows, :], weights, preferred_element_type=jnp.float32).astype(jnp.bfloat16)
        q_buf[k, rows, :] = result[:, :head]
        here = min(2 * tok - first, count)
        kv[0, k, pl.ds(first, here), :] = result[:here, head:]
        if here < count:
            kv[1, k, pl.ds(2 * tok - (count - here), count - here), :] = result[here:, head:]

    def share_kv(k, first, count):
        rows = pl.ds(first, count)
        for d in range(1, pairs):
            there = (k + d) % pairs
            start(kv.at[0, k, rows, :], kv.at[d, there, rows, :], kv_s, kv_r.at[d - 1, there], at_pair(d, 0))

    def attention(k, first, count):
        total = pairs * 2 * tok
        keys = kv[:, k, :, :head].reshape(total, head)
        values = kv[:, k, :, head:].reshape(total, head)
        query = q_buf[k, pl.ds(first, count), :]
        scores = lax.dot_general(query, keys, (((1,), (1,)), ((), ())), preferred_element_type=jnp.float32)
        scores = scores / math.sqrt(head)
        largest = jnp.max(scores, axis=1, keepdims=True)
        weights = jnp.exp(scores - largest)
        probs = (weights / jnp.sum(weights, axis=1, keepdims=True)).astype(jnp.bfloat16)
        return jnp.dot(probs, values, preferred_element_type=jnp.float32).astype(jnp.bfloat16)

    def att_cols(k):
        return pl.ds(pl.multiple_of((parity * pairs + k) * head, head), head)

    def send_att(k, count):
        rows = pl.ds(0, count)
        start(att_send.at[k, rows, :], att_mine.at[rows, att_cols(k)], at_s, at_r, mate)

    def drain(region, ssem):
        remote(region, region, ssem, at_r, sib).wait_send()

    spread_sends = 7 if square else 2 * chips - 1

    def drain_o(passed):
        drain(wq.at[0 : (n_sp * spread_sends + passed) * rows_o * width // (3 * head), :], o_s)

    def general():
        far_o = [spread_o(k, f) for k, f in far]

        def send_o(n):
            for k, f in far[n : n + 1]:
                pass_o(parity, 0, k, f, at_pair(k, f))

        def take_o(n):
            land_o(*far[n])
            far_o[n].begin()

        all_q[0].begin()
        near_o.begin()
        send_q()
        send_chunk(0)
        modulate()
        normalize(0, tok)
        all_q[0].relay()
        near_o.relay()
        send_chunk(1)
        for k in range(1, pairs):
            arrive(wq_rows(k, g), q_s, wz_r.at[k])
            all_q[k].begin()
        send_o(0)
        send_chunk(2)
        send_o(1)
        send_chunk(3)
        for n in range(2, len(far)):
            send_o(n)
        all_q[0].last()
        finish_q(0)
        project(0, 0, tok)
        share_kv(0, 0, tok)
        near_o.last()
        for k in range(1, pairs):
            all_q[k].relay()
        normalize_chunk(0)
        for k in range(1, pairs):
            all_q[k].last()
            finish_q(k)
            project(k, 0, tok)
            share_kv(k, 0, tok)
        take_o(0)
        take_o(1)
        for c in range(1, CHUNKS):
            normalize_chunk(c)
        for k in range(pairs):
            project(k, tok, tok)
            share_kv(k, tok, tok)
        far_o[0].relay()
        for n in range(2, len(far)):
            take_o(n)
        far_o[1].relay()
        far_o[0].last()
        for spread in far_o[2:]:
            spread.relay()
        far_o[1].last()
        for k in range(pairs):
            for d in range(1, pairs):
                arrive(kv.at[d, k], kv_s, kv_r.at[d - 1, k])
            att_send[k] = attention(k, tok, tok)
            send_att(k, tok)
            att_mine[:, att_cols(k)] = attention(k, 0, tok)
        for spread in far_o[2:]:
            spread.last()
        arrive(wo.at[0 : n_sp * head // 2, :], o_s, od_r)
        arrive(att_send, at_s, at_r)
        drain_o(n_sp - 1)
        for d in range(1, pairs):
            drain(kv.at[0], kv_s)
        drain(att_send, at_s)

    def along_line():
        far_a, far_b, far_c = spread_o(0, 1), spread_o(1, inner), spread_o(1, 1 - inner)
        all_q[0].begin()
        near_o.begin()
        send_q()
        send_chunk(0)

        @when_outer
        def _():
            pass_o(parity, 0, 0, 1, mate)
            for c in range(1, CHUNKS):
                send_chunk(c)

        modulate()
        normalize(0, tok)

        @when_inner
        def _():
            pass_o(parity, 0, 0, 1, mate)
            pass_o(parity, 0, 1, 1, at_pair(1, 1))

        all_q[0].relay()
        near_o.relay()
        arrive(wq_rows(1, g), q_s, wz_r.at[1])
        all_q[1].begin()

        @when_inner
        def _():
            for c in range(1, CHUNKS - 1):
                send_chunk(c)
            send_inner()

        normalize_chunk(0)
        all_q[0].last()
        finish_q(0)
        project(0, 0, tok)
        share_kv(0, 0, tok)
        near_o.last()
        land_o(0, 1)

        @when_inner
        def _():
            pass_o(1 - parity, 0, 1, 0, at_pair(1, 1))

        far_a.begin()
        normalize_chunk(1)

        @when_inner
        def _():
            land_o(1, 1)
            pass_o(1 - parity, 1, 1, 0, mate)
            land_o(1, 0)
            pass_o(parity, 1, 1, 1, mate)

        all_q[1].relay()
        far_a.relay()

        @when_inner
        def _():
            far_b.begin()
            far_c.begin()

        all_q[1].last()
        finish_q(1)
        project(1, 0, tok)
        share_kv(1, 0, tok)
        far_a.last()
        normalize_chunk(2)

        @when_outer
        def _():
            land_o(1, 0)
            far_b.begin()

        for k in range(pairs):
            project(k, tok, part_rows)
            share_kv(k, tok, part_rows)

        @when_outer
        def _():
            land_o(1, 1)
            far_c.begin()

        @when_inner
        def _():
            far_b.relay()
            land_chunk(CHUNKS - 1)
            arrive(lat.at[pl.ds(2 * tok, piece), :], lat_s, x_r.at[0])
            normalize(2 * tok - piece, 2 * piece)
            rows = pl.ds(2 * tok - piece, piece)
            for k in range(pairs):
                project(k, 2 * tok - piece, 2 * piece)
                start(kv.at[1, k, rows, :], kv.at[0, 1 - k, rows, :], kv_s, x_r.at[2 - k], at_pair(1, 0))
                share_kv(k, 2 * tok - piece, piece)

        @when_outer
        def _():
            far_b.relay()

        far_c.relay()
        far_b.last()
        far_c.last()
        for k in range(pairs):

            @when_inner
            def _():
                arrive(kv.at[1, k, pl.ds(0, tok + part_rows), :], kv_s, kv_r.at[0, k])
                there = pl.ds(pl.multiple_of((parity * pairs + 1 - k) * head, head), head)
                far_rows = pl.ds(part_rows, piece)
                att_send[k] = attention(k, tok, tok)
                send_att(k, tok)
                att_far[k] = attention(k, 2 * tok, piece)
                start(att_far.at[k], att_mine.at[far_rows, there], at_s, x_r.at[3], at_pair(1, 1))

            @when_outer
            def _():
                arrive(kv.at[1, k], kv_s, kv_r.at[0, k])
                arrive(kv.at[0, k, pl.ds(2 * tok - piece, piece), :], kv_s, x_r.at[1 + k])
                att_send[k, 0:part_rows] = attention(k, tok, part_rows)
                send_att(k, part_rows)

            att_mine[:, att_cols(k)] = attention(k, 0, tok)
        arrive(wo.at[0 : n_sp * head // 2, :], o_s, od_r)

        @when_inner
        def _():
            arrive(att_send.at[:, pl.ds(0, part_rows), :], at_s, at_r)
            arrive(att_far, at_s, x_r.at[3])
            drain_o(5)
            drain(lat.at[0 : pairs * (2 * tok + piece) * 2 * head // width, :], kv_s)
            drain(q_buf.at[:, pl.ds(0, tok + piece), :], at_s)

        @when_outer
        def _():
            arrive(att_send, at_s, at_r)
            drain_o(1)
            drain(kv.at[0, :, pl.ds(0, tok + part_rows), :], kv_s)
            drain(att_send.at[:, pl.ds(0, part_rows), :], at_s)

    if line:
        along_line()
    else:
        general()
    drain(wq.at[0 : (pairs * spread_sends + pairs - 1) * rows_q, :], q_s)
    drain(lat.at[0:tok, :], lat_s)


def project_out(att, wo, mod, out_hbm, out_buf, sems):
    width = wo.shape[1]
    step = width // sems.shape[0]
    outs = []
    for i in range(sems.shape[0]):
        cols = slice(i * step, (i + 1) * step)
        total = jnp.dot(att[...], wo[:, cols], preferred_element_type=jnp.float32)
        gate = mod[0:1, 2 * width + i * step : 2 * width + (i + 1) * step]
        out_buf[:, cols] = (gate * total).astype(jnp.bfloat16)
        outs.append(pltpu.make_async_copy(out_buf.at[:, cols], out_hbm.at[0, :, cols], sems.at[i]))
        outs[i].start()
    for copy in outs:
        copy.wait()


def on_device(n_grp, n_sp, latents, timestep, w_mod, w_qkv, w_out):
    _, tok, width = latents.shape
    head = w_qkv.shape[2] // 3
    pairs, chips = n_sp // 2, n_grp // 2
    dma = pltpu.SemaphoreType.DMA
    bf16 = jnp.bfloat16
    anywhere = pl.BlockSpec(memory_space=pl.ANY)
    vmem = pl.BlockSpec(memory_space=pltpu.VMEM)
    args = [pltpu.with_memory_space_constraint(a, pltpu.HBM) for a in (latents, w_mod, w_qkv, w_out)]
    att, wo, mod = pl.pallas_call(
        functools.partial(kernel, n_grp, n_sp),
        out_shape=[
            pltpu.VMEM((tok, n_sp * head), bf16),
            pltpu.VMEM((n_sp * head, width), bf16),
            pltpu.VMEM((8, w_mod.shape[1]), jnp.float32),
        ],
        in_specs=[pl.BlockSpec(memory_space=pltpu.SMEM)] + [anywhere] * 4,
        out_specs=[vmem] * 3,
        scratch_shapes=[
            pltpu.VMEM((2 * tok + tok // CHUNKS, width), bf16),
            pltpu.VMEM(w_mod.shape, bf16),
            pltpu.VMEM((2 * tok + tok // CHUNKS, width), bf16),
            pltpu.VMEM((pairs * width, 3 * head), bf16),
            pltpu.VMEM((pairs, 2 * tok + tok // CHUNKS, head), bf16),
            pltpu.VMEM((pairs, pairs, 2 * tok, 2 * head), bf16),
            pltpu.VMEM((pairs, tok, head), bf16),
            pltpu.VMEM((pairs, tok // CHUNKS, head), bf16),
            dma((4,)),
            dma,
            dma,
            dma,
            dma,
            dma,
            dma((pairs,)),
            dma((pairs, max(chips - 1, 4))),
            dma((pairs,)),
            dma((n_sp,)),
            dma((n_sp, max(chips - 1, 4))),
            dma,
            dma((CHUNKS,)),
            dma((max(pairs - 1, 1), pairs)),
            dma,
            dma((4,)),
        ],
        compiler_params=pltpu.CompilerParams(collective_id=0, has_side_effects=True, vmem_limit_bytes=LIMIT),
    )(timestep, *args)
    return pl.pallas_call(
        project_out,
        out_shape=jax.ShapeDtypeStruct(latents.shape, bf16),
        in_specs=[vmem] * 3,
        out_specs=anywhere,
        scratch_shapes=[pltpu.VMEM((tok, width), bf16), dma((max(width // 512, 1),))],
        compiler_params=pltpu.CompilerParams(vmem_limit_bytes=8 * 2**20),
    )(att, wo, mod)


def solution(mesh):
    placed = (P("grp", "sp", None), P("grp"), P(), P("sp", "grp", None), P("sp", "grp", None))
    body = functools.partial(on_device, mesh.shape["grp"], mesh.shape["sp"])
    return jax.shard_map(
        body, mesh=mesh, in_specs=placed, out_specs=P("grp", "sp", None), check_vma=False
    )
```

time: 54.2 us -> 51.6 us (0.952)
  Pallas kernels: 53.4 us -> 50.8 us
    pallas_call x1, Pallas kernels: 52.1 us -> 49.5 us  [on_device(): pl.pallas_call(functools.partial(kernel, n_grp, n_sp), out_shape=[pltpu.V...]
where the time goes in v2:
time: 51.6 us; the launch traced here: 51.5 us
  Pallas kernels  50.8 us (98%)
  between operations  0.66 us (1%)
    pallas_call x1, Pallas kernels, on_device(): pl.pallas_call(functools.partial(kernel, n_grp, n_sp), out_shape=[pltpu.V...  49.5 us
    pallas_call x1, Pallas kernels, on_device(): pl.pallas_call(project_out, out_shape=jax.ShapeDtypeStruct(latents.shape,...  1.3 us

profile of v2, /device:TPU:0, one launch (start us, length us, event | category | flops | bytes accessed | tf_op | source)
XLA Modules:
  0.0 51.5 jit_solution(2676440852985213873)
XLA Ops:
  0.7 49.5 %shard_map.55 = (bf16[128,512]{1,0:T(8,128)(2,1)S(1)}, bf16[512,3072]{1,0:T(8,128)(2,1)S(1)}, f32[8,9216]{1,0:T(8,128)S(1)}) custom-call(s32[1]{0:T(128)S(6)} %copy.6.step_now, bf16[1,128,3072]{2,1,0:T(8,128)(2,1)} %lat_hbm.1, bf16[256,9216]{1,0:T(8,128)(2,1)} %wmod_hbm.1, bf16[1,384,384]{2,1,0:T(8,128)(2,1)} %wqkv_hbm.1, bf16[1,16,3072]{2,1,0:T(8,128)(2,1)} %wout_hbm.1), custom_call_target="tpu_custom_call" | custom-call | tf_op jit(solution)/shard_map/pallas_call | solution.py:538
  50.1 1.3 %shard_map.56 = bf16[1,128,3072]{2,1,0:T(8,128)(2,1)} custom-call(bf16[128,512]{1,0:T(8,128)(2,1)S(1)} %get-tuple-element.8.att, bf16[512,3072]{1,0:T(8,128)(2,1)S(1)} %get-tuple-element.9.wo, f32[8,9216]{1,0:T(8,128)S(1)} %get-tuple-element.10.mod), custom_call_target="tpu_custom_call" | custom-call | tf_op jit(solution)/shard_map/pallas_call | solution.py:575

commit v3 on v2

--- a/solution.py
+++ b/solution.py
@@ -55,6 +55,7 @@
     kv_r,
     at_r,
     x_r,
+    twin_in,
 ):
     g = lax.axis_index("grp")
     s = lax.axis_index("sp")
@@ -97,11 +98,29 @@
         first = (par * pairs + k) * head + owner * rows_o
         return wo.at[pl.ds(pl.multiple_of(first, rows_o), rows_o), :]
 
+    square = chips == 4
+    near_x = chip // 2 * 2 + 1 - chip % 2
+    near_y = (chip + 2) % 4
+    corner = (near_x + 2) % 4
+    to_x, to_y = (near_x * 2 + core, s), (near_y * 2 + core, s)
+
+    def tell(sem, device):
+        pl.semaphore_signal(sem, inc=1, device_id=device, device_id_type=MESH)
+
     barrier = pltpu.get_barrier_semaphore()
-    peers = [sib] + [at_chip(c) for c in range(1, chips)]
-    peers += [at_pair(k, f) for k in range(pairs) for f in range(2) if (k, f) != (0, 0)]
+    peers = [sib] + ([to_x, to_y] if square else [at_chip(c) for c in range(1, chips)])
+    if line:
+        peers.append(mate)
+    else:
+        peers += [at_pair(k, f) for k in range(pairs) for f in range(2) if (k, f) != (0, 0)]
     for peer in peers:
-        pl.semaphore_signal(barrier, inc=1, device_id=peer, device_id_type=MESH)
+        tell(barrier, peer)
+    if line:
+
+        @when_inner
+        def _():
+            tell(barrier, at_pair(1, 1))
+
     local = [
         pltpu.make_async_copy(wqkv_hbm.at[0], wq_rows(0, g), loc_sem.at[0]),
         pltpu.make_async_copy(wout_hbm.at[0], wo_rows(parity, 0, g), loc_sem.at[1]),
@@ -112,8 +131,20 @@
         copy.start()
     local[0].wait()
     local[1].wait()
-    local[2].wait()
-    pl.semaphore_wait(barrier, len(peers))
+    if line:
+
+        @when_inner
+        def _():
+            pl.semaphore_wait(barrier, len(peers) + 1)
+            tell(twin_in, mate)
+            tell(twin_in, at_pair(1, 1))
+
+        @when_outer
+        def _():
+            pl.semaphore_wait(barrier, len(peers))
+
+    else:
+        pl.semaphore_wait(barrier, len(peers))
 
     def start(src, dst, ssem, rsem, device):
         remote(src, dst, ssem, rsem, device).start()
@@ -121,11 +152,6 @@
     def arrive(region, ssem, rsem):
         remote(region, region, ssem, rsem, sib).wait_recv()
 
-    square = chips == 4
-    near_x = chip // 2 * 2 + 1 - chip % 2
-    near_y = (chip + 2) % 4
-    corner = (near_x + 2) % 4
-    to_x, to_y = (near_x * 2 + core, s), (near_y * 2 + core, s)
     others = [near_x, near_y, corner] if square else [(chip + chips - c) % chips for c in range(1, chips)]
 
     def q_part(k, owner, half):
@@ -185,6 +211,21 @@
         whole, part = functools.partial(wq_rows, k), functools.partial(q_part, k)
         return Spread(k, whole, part, q_s, wx_r, wd_r.at[k])
 
+    def spread_cols(k, slot, first, count):
+        def cut(region):
+            return region.at[:, first : first + count]
+
+        def whole(owner):
+            return cut(wq_rows(k, owner))
+
+        def part(owner, half):
+            return cut(q_part(k, owner, half))
+
+        return Spread(slot, whole, part, q_s, wx_r, wd_r.at[slot])
+
+    def finish_cols(k, slot, first, count):
+        arrive(wq.at[k * width : k * width + width // 2, first : first + count], q_s, wd_r.at[slot])
+
     def finish_q(k):
         arrive(wq.at[k * width : k * width + width // 2, :], q_s, wd_r.at[k])
 
@@ -253,11 +294,26 @@
         rows = pl.ds(first, count)
         weights = wq[k * width : (k + 1) * width, :]
         result = jnp.dot(normed[rows, :], weights, preferred_element_type=jnp.float32).astype(jnp.bfloat16)
-        q_buf[k, rows, :] = result[:, :head]
         here = min(2 * tok - first, count)
+        q_buf[k, pl.ds(first, here), :] = result[:here, :head]
         kv[0, k, pl.ds(first, here), :] = result[:here, head:]
         if here < count:
+            q_buf[k, pl.ds(3 * tok - (count - here), count - here), :] = result[here:, :head]
             kv[1, k, pl.ds(2 * tok - (count - here), count - here), :] = result[here:, head:]
+
+    def project_part(k, first, count, is_q):
+        rows = pl.ds(first, count)
+        weights = wq[k * width : (k + 1) * width, 0:head] if is_q else wq[k * width : (k + 1) * width, head:]
+        result = jnp.dot(normed[rows, :], weights, preferred_element_type=jnp.float32).astype(jnp.bfloat16)
+        here = min(2 * tok - first, count)
+        if is_q:
+            q_buf[k, pl.ds(first, here), :] = result[:here]
+        else:
+            kv[0, k, pl.ds(first, here), :] = result[:here]
+        if here < count and is_q:
+            q_buf[k, pl.ds(3 * tok - (count - here), count - here), :] = result[here:]
+        elif here < count:
+            kv[1, k, pl.ds(2 * tok - (count - here), count - here), :] = result[here:]
 
     def share_kv(k, first, count):
         rows = pl.ds(first, count)
@@ -271,18 +327,13 @@
         values = kv[:, k, :, head:].reshape(total, head)
         query = q_buf[k, pl.ds(first, count), :]
         scores = lax.dot_general(query, keys, (((1,), (1,)), ((), ())), preferred_element_type=jnp.float32)
-        scores = scores / math.sqrt(head)
         largest = jnp.max(scores, axis=1, keepdims=True)
-        weights = jnp.exp(scores - largest)
-        probs = (weights / jnp.sum(weights, axis=1, keepdims=True)).astype(jnp.bfloat16)
-        return jnp.dot(probs, values, preferred_element_type=jnp.float32).astype(jnp.bfloat16)
-
-    def att_cols(k):
-        return pl.ds(pl.multiple_of((parity * pairs + k) * head, head), head)
-
-    def send_att(k, count):
-        rows = pl.ds(0, count)
-        start(att_send.at[k, rows, :], att_mine.at[rows, att_cols(k)], at_s, at_r, mate)
+        weights = jnp.exp((scores - largest) * (1.0 / math.sqrt(head)))
+        mixed = jnp.dot(weights.astype(jnp.bfloat16), values, preferred_element_type=jnp.float32)
+        return (mixed / jnp.sum(weights, axis=1, keepdims=True)).astype(jnp.bfloat16)
+
+    def send_att(k):
+        start(att_send.at[k], att_mine.at[parity * pairs + k], at_s, at_r, mate)
 
     def drain(region, ssem):
         remote(region, region, ssem, at_r, sib).wait_send()
@@ -306,6 +357,7 @@
         all_q[0].begin()
         near_o.begin()
         send_q()
+        local[2].wait()
         send_chunk(0)
         modulate()
         normalize(0, tok)
@@ -353,8 +405,8 @@
             for d in range(1, pairs):
                 arrive(kv.at[d, k], kv_s, kv_r.at[d - 1, k])
             att_send[k] = attention(k, tok, tok)
-            send_att(k, tok)
-            att_mine[:, att_cols(k)] = attention(k, 0, tok)
+            send_att(k)
+            att_mine[parity * pairs + k] = attention(k, 0, tok)
         for spread in far_o[2:]:
             spread.last()
         arrive(wo.at[0 : n_sp * head // 2, :], o_s, od_r)
@@ -366,142 +418,205 @@
 
     def along_line():
         far_a, far_b, far_c = spread_o(0, 1), spread_o(1, inner), spread_o(1, 1 - inner)
+        cols = {"kv": (1, head, 2 * head), "q": (2, 0, head)}
+        other = {name: spread_cols(1, *cut) for name, cut in cols.items()}
+        late = tok + 2 * piece
+
+        def send_other(name):
+            slot, first, count = cols[name]
+            source, target = wq_rows(0, g), wq_rows(1, g)
+            width_of = slice(first, first + count)
+            start(source.at[:, width_of], target.at[:, width_of], q_s, wz_r.at[slot], at_pair(1, 0))
+
+        def take_other(name):
+            slot, first, count = cols[name]
+            arrive(wq_rows(1, g).at[:, first : first + count], q_s, wz_r.at[slot])
+            other[name].begin()
+
         all_q[0].begin()
         near_o.begin()
-        send_q()
-        send_chunk(0)
-
-        @when_outer
-        def _():
+        local[2].wait()
+
+        @when_inner
+        def _():
+            pl.semaphore_wait(twin_in, 1)
+            send_other("kv")
+
+        @when_outer
+        def _():
+            send_chunk(0)
+            pl.semaphore_wait(twin_in, 1)
+            send_other("kv")
             pass_o(parity, 0, 0, 1, mate)
+
+        modulate()
+        normalize(0, tok)
+
+        @when_inner
+        def _():
+            send_chunk(0)
+
+        all_q[0].relay()
+        send_other("q")
+
+        @when_inner
+        def _():
+            pass_o(parity, 0, 0, 1, mate)
+            pass_o(parity, 0, 1, 1, at_pair(1, 1))
+
+        @when_outer
+        def _():
             for c in range(1, CHUNKS):
                 send_chunk(c)
 
-        modulate()
-        normalize(0, tok)
-
-        @when_inner
-        def _():
-            pass_o(parity, 0, 0, 1, mate)
-            pass_o(parity, 0, 1, 1, at_pair(1, 1))
-
-        all_q[0].relay()
+        take_other("kv")
         near_o.relay()
-        arrive(wq_rows(1, g), q_s, wz_r.at[1])
-        all_q[1].begin()
-
-        @when_inner
-        def _():
-            for c in range(1, CHUNKS - 1):
-                send_chunk(c)
-            send_inner()
+
+        @when_inner
+        def _():
+            send_chunk(1)
+            send_chunk(2)
+            land_o(0, 1)
+            pass_o(1 - parity, 0, 1, 0, at_pair(1, 1))
 
         normalize_chunk(0)
         all_q[0].last()
         finish_q(0)
         project(0, 0, tok)
-        share_kv(0, 0, tok)
+
+        @when_outer
+        def _():
+            share_kv(0, 0, tok)
+
+        @when_inner
+        def _():
+            land_o(1, 1)
+            pass_o(1 - parity, 1, 1, 0, mate)
+
+        take_other("q")
         near_o.last()
-        land_o(0, 1)
-
-        @when_inner
-        def _():
-            pass_o(1 - parity, 0, 1, 0, at_pair(1, 1))
+        other["kv"].relay()
+
+        @when_inner
+        def _():
+            land_o(1, 0)
+            pass_o(parity, 1, 1, 1, mate)
+            send_inner()
+
+        @when_outer
+        def _():
+            land_o(0, 1)
 
         far_a.begin()
         normalize_chunk(1)
-
-        @when_inner
-        def _():
-            land_o(1, 1)
-            pass_o(1 - parity, 1, 1, 0, mate)
-            land_o(1, 0)
-            pass_o(parity, 1, 1, 1, mate)
-
-        all_q[1].relay()
-        far_a.relay()
+        project(0, tok, 2 * piece)
+
+        @when_outer
+        def _():
+            share_kv(0, tok, 2 * piece)
+
+        other["q"].relay()
 
         @when_inner
         def _():
             far_b.begin()
             far_c.begin()
-
-        all_q[1].last()
-        finish_q(1)
-        project(1, 0, tok)
-        share_kv(1, 0, tok)
-        far_a.last()
-        normalize_chunk(2)
+            normalize_chunk(2)
+            share_kv(0, 0, late)
+
+        other["kv"].last()
+        finish_cols(1, *cols["kv"])
+        project_part(1, 0, late, False)
+
+        share_kv(1, 0, late)
 
         @when_outer
         def _():
             land_o(1, 0)
             far_b.begin()
 
-        for k in range(pairs):
-            project(k, tok, part_rows)
-            share_kv(k, tok, part_rows)
-
-        @when_outer
-        def _():
+        far_a.relay()
+        other["q"].last()
+        finish_cols(1, *cols["q"])
+
+        @when_inner
+        def _():
+            land_chunk(3)
+            arrive(lat.at[pl.ds(2 * tok, piece), :], lat_s, x_r.at[0])
+            normalize(late + piece, 2 * piece)
+            far_b.relay()
+            rows = pl.ds(2 * tok - piece, piece)
+
+            def pass_kv(k):
+                start(kv.at[1, k, rows, :], kv.at[0, 1 - k, rows, :], kv_s, x_r.at[2 - k], at_pair(1, 0))
+                share_kv(k, late, 2 * piece)
+
+            project(0, late, 3 * piece)
+            pass_kv(0)
+            project_part(1, late, 3 * piece, False)
+            pass_kv(1)
+            far_c.relay()
+            project_part(1, 0, 2 * tok + piece, True)
+
+        @when_outer
+        def _():
+            normalize_chunk(2)
+            rows, there = pl.ds(tok, part_rows), pl.ds(2 * tok, part_rows)
+
+            def pass_query(k):
+                start(q_buf.at[k, rows, :], q_buf.at[1 - k, there, :], at_s, x_r.at[2 - k], at_pair(1, 0))
+
+            project(0, late, piece)
+            share_kv(0, late, piece)
+            pass_query(0)
+            project_part(1, late, piece, False)
+            share_kv(1, late, piece)
+            project_part(1, 0, late + piece, True)
+            pass_query(1)
             land_o(1, 1)
             far_c.begin()
-
-        @when_inner
-        def _():
             far_b.relay()
-            land_chunk(CHUNKS - 1)
-            arrive(lat.at[pl.ds(2 * tok, piece), :], lat_s, x_r.at[0])
-            normalize(2 * tok - piece, 2 * piece)
-            rows = pl.ds(2 * tok - piece, piece)
-            for k in range(pairs):
-                project(k, 2 * tok - piece, 2 * piece)
-                start(kv.at[1, k, rows, :], kv.at[0, 1 - k, rows, :], kv_s, x_r.at[2 - k], at_pair(1, 0))
-                share_kv(k, 2 * tok - piece, piece)
-
-        @when_outer
-        def _():
-            far_b.relay()
-
-        far_c.relay()
+            far_c.relay()
+
+        far_a.last()
         far_b.last()
         far_c.last()
-        for k in range(pairs):
-
-            @when_inner
-            def _():
+
+        @when_inner
+        def _():
+            for k in range(pairs):
                 arrive(kv.at[1, k, pl.ds(0, tok + part_rows), :], kv_s, kv_r.at[0, k])
-                there = pl.ds(pl.multiple_of((parity * pairs + 1 - k) * head, head), head)
-                far_rows = pl.ds(part_rows, piece)
-                att_send[k] = attention(k, tok, tok)
-                send_att(k, tok)
-                att_far[k] = attention(k, 2 * tok, piece)
-                start(att_far.at[k], att_mine.at[far_rows, there], at_s, x_r.at[3], at_pair(1, 1))
-
-            @when_outer
-            def _():
+                arrive(q_buf.at[k, pl.ds(2 * tok, part_rows), :], at_s, x_r.at[1 + k])
+            for k in range(pairs):
+                result = attention(k, tok, 2 * tok)
+                att_send[k] = result[:tok]
+                att_far[k] = result[tok:]
+            for k in range(pairs):
+                send_att(k)
+                start(att_far.at[k], att_mine.at[parity * pairs + 1 - k], at_s, at_r, at_pair(1, 1))
+
+        @when_outer
+        def _():
+            for k in range(pairs):
                 arrive(kv.at[1, k], kv_s, kv_r.at[0, k])
                 arrive(kv.at[0, k, pl.ds(2 * tok - piece, piece), :], kv_s, x_r.at[1 + k])
-                att_send[k, 0:part_rows] = attention(k, tok, part_rows)
-                send_att(k, part_rows)
-
-            att_mine[:, att_cols(k)] = attention(k, 0, tok)
+
+        for k in range(pairs):
+            att_mine[parity * pairs + k] = attention(k, 0, tok)
         arrive(wo.at[0 : n_sp * head // 2, :], o_s, od_r)
-
-        @when_inner
-        def _():
-            arrive(att_send.at[:, pl.ds(0, part_rows), :], at_s, at_r)
-            arrive(att_far, at_s, x_r.at[3])
+        arrive(att_send, at_s, at_r)
+
+        @when_inner
+        def _():
             drain_o(5)
             drain(lat.at[0 : pairs * (2 * tok + piece) * 2 * head // width, :], kv_s)
-            drain(q_buf.at[:, pl.ds(0, tok + piece), :], at_s)
-
-        @when_outer
-        def _():
-            arrive(att_send, at_s, at_r)
+            drain(q_buf.at[:, 0 : 2 * tok, :], at_s)
+
+        @when_outer
+        def _():
             drain_o(1)
             drain(kv.at[0, :, pl.ds(0, tok + part_rows), :], kv_s)
-            drain(att_send.at[:, pl.ds(0, part_rows), :], at_s)
+            drain(q_buf.at[:, 0:part_rows, :], at_s)
 
     if line:
         along_line()
@@ -514,10 +629,11 @@
 def project_out(att, wo, mod, out_hbm, out_buf, sems):
     width = wo.shape[1]
     step = width // sems.shape[0]
+    mixed = jnp.concatenate([att[i] for i in range(att.shape[0])], axis=1)
     outs = []
     for i in range(sems.shape[0]):
         cols = slice(i * step, (i + 1) * step)
-        total = jnp.dot(att[...], wo[:, cols], preferred_element_type=jnp.float32)
+        total = jnp.dot(mixed, wo[:, cols], preferred_element_type=jnp.float32)
         gate = mod[0:1, 2 * width + i * step : 2 * width + (i + 1) * step]
         out_buf[:, cols] = (gate * total).astype(jnp.bfloat16)
         outs.append(pltpu.make_async_copy(out_buf.at[:, cols], out_hbm.at[0, :, cols], sems.at[i]))
@@ -538,7 +654,7 @@
     att, wo, mod = pl.pallas_call(
         functools.partial(kernel, n_grp, n_sp),
         out_shape=[
-            pltpu.VMEM((tok, n_sp * head), bf16),
+            pltpu.VMEM((n_sp, tok, head), bf16),
             pltpu.VMEM((n_sp * head, width), bf16),
             pltpu.VMEM((8, w_mod.shape[1]), jnp.float32),
         ],
@@ -549,19 +665,19 @@
             pltpu.VMEM(w_mod.shape, bf16),
             pltpu.VMEM((2 * tok + tok // CHUNKS, width), bf16),
             pltpu.VMEM((pairs * width, 3 * head), bf16),
-            pltpu.VMEM((pairs, 2 * tok + tok // CHUNKS, head), bf16),
+            pltpu.VMEM((pairs, 3 * tok, head), bf16),
             pltpu.VMEM((pairs, pairs, 2 * tok, 2 * head), bf16),
             pltpu.VMEM((pairs, tok, head), bf16),
-            pltpu.VMEM((pairs, tok // CHUNKS, head), bf16),
+            pltpu.VMEM((pairs, tok, head), bf16),
             dma((4,)),
             dma,
             dma,
             dma,
             dma,
             dma,
-            dma((pairs,)),
-            dma((pairs, max(chips - 1, 4))),
-            dma((pairs,)),
+            dma((max(pairs, 3),)),
+            dma((max(pairs, 3), max(chips - 1, 4))),
+            dma((max(pairs, 3),)),
             dma((n_sp,)),
             dma((n_sp, max(chips - 1, 4))),
             dma,
@@ -569,6 +685,7 @@
             dma((max(pairs - 1, 1), pairs)),
             dma,
             dma((4,)),
+            pltpu.SemaphoreType.REGULAR,
         ],
         compiler_params=pltpu.CompilerParams(collective_id=0, has_side_effects=True, vmem_limit_bytes=LIMIT),
     )(timestep, *args)

time: 51.6 us -> 47.6 us (0.922)
  Pallas kernels: 50.8 us -> 46.8 us
    pallas_call x1, Pallas kernels: 49.5 us -> 45.5 us  [on_device(): pl.pallas_call(functools.partial(kernel, n_grp, n_sp), out_shape=[pltpu.V...]
where the time goes in v3:
time: 47.6 us; the launch traced here: 47.5 us
  Pallas kernels  46.8 us (98%)
  between operations  0.66 us (1%)
    pallas_call x1, Pallas kernels, on_device(): pl.pallas_call(functools.partial(kernel, n_grp, n_sp), out_shape=[pltpu.V...  45.5 us
    pallas_call x1, Pallas kernels, on_device(): pl.pallas_call(project_out, out_shape=jax.ShapeDtypeStruct(latents.shape,...  1.31 us

profile of v3, /device:TPU:0, one launch (start us, length us, event | category | flops | bytes accessed | tf_op | source)
XLA Modules:
  0.0 47.5 jit_solution(317566896457356761)
XLA Ops:
  0.7 45.5 %shard_map.55 = (bf16[4,128,128]{2,1,0:T(8,128)(2,1)S(1)}, bf16[512,3072]{1,0:T(8,128)(2,1)S(1)}, f32[8,9216]{1,0:T(8,128)S(1)}) custom-call(s32[1]{0:T(128)S(6)} %copy.6.step_now, bf16[1,128,3072]{2,1,0:T(8,128)(2,1)} %lat_hbm.1, bf16[256,9216]{1,0:T(8,128)(2,1)} %wmod_hbm.1, bf16[1,384,384]{2,1,0:T(8,128)(2,1)} %wqkv_hbm.1, bf16[1,16,3072]{2,1,0:T(8,128)(2,1)} %wout_hbm.1), custom_call_target="tpu_custom_call" | custom-call | tf_op jit(solution)/shard_map/pallas_call | solution.py:654
  46.1 1.3 %shard_map.56 = bf16[1,128,3072]{2,1,0:T(8,128)(2,1)} custom-call(bf16[4,128,128]{2,1,0:T(8,128)(2,1)S(1)} %get-tuple-element.8.att, bf16[512,3072]{1,0:T(8,128)(2,1)S(1)} %get-tuple-element.9.wo, f32[8,9216]{1,0:T(8,128)S(1)} %get-tuple-element.10.mod), custom_call_target="tpu_custom_call" | custom-call | tf_op jit(solution)/shard_map/pallas_call | solution.py:692
